TPU v7x, 32 devices: a whole 2x2x4 slice. The times are simulated.
32 devices in a mesh: rep: 2 (over y), tp: 4 (over z), sub: 4 (over x, core).
Axes of the slice: x: 2, y: 2, z: 4, core: 2. Of those that a mesh axis runs over, the one named last changes fastest.
Arguments:
- hidden_in: bfloat16 [128, 6144], P(('rep', 'sub'), 'tp'), parts along dimension 0, may hold values from -128 to 128
- query: bfloat16 [128, 6144], P(('rep', 'sub'), 'tp'), parts along dimension 0, may hold values from -128 to 128
- key_new: bfloat16 [128, 1024], P(('rep', 'sub'), 'tp'), parts along dimension 0, may hold values from -8 to 8
- value_new: bfloat16 [128, 1024], P(('rep', 'sub'), 'tp'), parts along dimension 0, may hold values from -6 to 6
- key_cache: bfloat16 [128, 128, 1024], P(('rep', 'sub'), 'tp'), parts along dimension 0, may hold values from -8 to 8
- value_cache: bfloat16 [128, 128, 1024], P(('rep', 'sub'), 'tp'), parts along dimension 0, may hold values from -6 to 6
- lengths: int32 [128], P(('rep', 'sub')), parts along dimension 0, may hold values from 2 to 128
- out_weight: bfloat16 [6144, 6144], P('sub', 'tp'), may hold values from -0.078125 to 0.078125
- norm_gain: bfloat16 [6144], P('tp'), may hold values from 0.099609375 to 1.8984375
- router_weight: bfloat16 [6144, 4], P('tp'), may hold values from -0.078125 to 0.078125
- routes: int32 [128, 2], P(('rep', 'sub')), parts along dimension 0, may hold values from 0 to 3, all different within a row; in each aligned block of 16 rows (0 to 15, 16 to 31, ...) at most 12 rows name the same one
- gate_weight: bfloat16 [4, 6144, 8192], P('sub', None, 'tp'), may hold values from -0.078125 to 0.078125
- up_weight: bfloat16 [4, 6144, 8192], P('sub', None, 'tp'), may hold values from -0.078125 to 0.078125
- down_weight: bfloat16 [4, 8192, 6144], P('sub', 'tp'), may hold values from -0.09375 to 0.09375
Outputs:
- layer_out: bfloat16 [128, 6144], P(('rep', 'sub'), 'tp'), parts along dimension 0
There are 2 independent parts, one for each index of `rep`. A program takes and returns all parts, laid end to end along the dimension named above; an argument that names none is the same for every part. Nothing has to cross between parts.
Inputs may be any that keep to these rules, and one draw needn't show every extreme that they name: `routes`: the two experts of a row differ; within the 16 rows of one index of sub, no expert is named by more than 12 rows, a bound that some such block reaches.
All inputs are finite; a program needn't handle non-finite values.
Results may differ from a plain program's by a relative error of at most 0.0075.
Values may be sent and summed in bfloat16 or wider, within the bound.
A program may use at most 128 MiB of HBM per device.

v0:
```python
import jax
import jax.numpy as jnp
from jax import lax
from jax.sharding import PartitionSpec as P

D = 6144
H = 48
KVH = 8
HD = 128
E = 4


def combined_all(value, axis, combine):
    everything = jax.tree.map(lambda part: lax.all_gather(part, axis), value)
    first = jax.tree.map(lambda part: part[0], everything)

    def hop(k, so_far):
        return combine(so_far, jax.tree.map(lambda part: part[k], everything))

    return lax.fori_loop(1, lax.axis_size(axis), hop, first)


def join_softmax(first, second):
    joined = jnp.maximum(first[0], second[0])
    first_scale = jnp.exp(first[0] - joined)
    second_scale = jnp.exp(second[0] - joined)
    totals = first[1] * first_scale + second[1] * second_scale
    summed = first[2] * first_scale[..., None] + second[2] * second_scale[..., None]
    return (joined, totals, summed)


def on_device(
    hidden_in,
    query,
    key_new,
    value_new,
    key_cache,
    value_cache,
    lengths,
    out_weight,
    norm_gain,
    router_weight,
    routes,
    gate_weight,
    up_weight,
    down_weight,
):
    seq_rows = hidden_in.shape[0]
    feat_width = hidden_in.shape[1]
    group_size = H // KVH
    scale_factor = 1.0 / HD**0.5
    local_len = key_cache.shape[1]
    all_query, all_key, all_value = (
        lax.all_gather(query, "tp", axis=1, tiled=True),
        lax.all_gather(key_new, "tp", axis=1, tiled=True),
        lax.all_gather(value_new, "tp", axis=1, tiled=True),
    )
    query_rows = all_query.reshape(seq_rows, KVH, group_size, HD)
    cached_keys = key_cache.reshape(seq_rows, local_len, KVH, HD)
    cached_values = value_cache.reshape(seq_rows, local_len, KVH, HD).astype(jnp.float32)
    scores = (
        jnp.einsum("bkgd,bpkd->bkgp", query_rows, cached_keys, preferred_element_type=jnp.float32)
        * scale_factor
    )
    positions = lax.axis_index("tp") * local_len + jnp.arange(local_len, dtype=jnp.int32)
    valid = positions[None, :] < lengths[:, None]
    scores = jnp.where(valid[:, None, None, :], scores, -jnp.inf)
    owned_part = (
        jnp.einsum(
            "zyqn,zyn->zyq",
            query_rows,
            all_key.reshape(seq_rows, KVH, HD),
            preferred_element_type=jnp.float32,
        )
        * scale_factor
    )
    local_max = jnp.maximum(jnp.max(scores, axis=-1), owned_part)
    weights = jnp.exp(scores - local_max[..., None])
    partial_total = jnp.sum(weights, axis=-1)
    local_summed = jnp.einsum("bkgp,bpkd->bkgd", weights, cached_values)
    run_max, total, summed = combined_all(
        (local_max, partial_total, local_summed), "tp", join_softmax
    )
    own_weight = jnp.exp(owned_part - run_max)
    total = total + own_weight
    new_values = all_value.reshape(seq_rows, KVH, 1, HD).astype(jnp.float32)
    summed = summed + own_weight[..., None] * new_values
    attn = (summed / total[..., None]).reshape(seq_rows, H * HD).astype(jnp.bfloat16)
    all_rows_attn = lax.all_to_all(attn, "sub", split_axis=1, concat_axis=0, tiled=True)
    partial_proj = jnp.dot(all_rows_attn, out_weight, preferred_element_type=jnp.float32)
    projected = lax.psum_scatter(partial_proj, "sub", scatter_dimension=0, tiled=True)
    resid = hidden_in.astype(jnp.float32) + projected
    gain_full = norm_gain.astype(jnp.float32)[None, :]
    router_full = router_weight.astype(jnp.float32)
    squares = lax.psum(jnp.sum(resid * resid, axis=-1), "tp")
    root = jnp.sqrt(squares / D + 1e-05)
    normed = resid / root[:, None] * gain_full
    logits = lax.psum(jnp.dot(normed, router_full, precision=lax.Precision.HIGHEST), "tp")
    normed_low = normed.astype(jnp.bfloat16)
    expert_ids = jnp.arange(E, dtype=jnp.int32)[None, :]
    first_hot = (routes[:, 0:1] == expert_ids).astype(jnp.float32)
    second_hot = (routes[:, 1:2] == expert_ids).astype(jnp.float32)
    first_logit = jnp.sum(logits * first_hot, axis=-1)
    second_logit = jnp.sum(logits * second_hot, axis=-1)
    first_weight = 1.0 / (1.0 + jnp.exp(second_logit - first_logit))
    second_weight = 1.0 / (1.0 + jnp.exp(first_logit - second_logit))
    dense = first_weight[:, None] * first_hot + second_weight[:, None] * second_hot
    gate_local = gate_weight[0]
    up_local = up_weight[0]
    down_local = down_weight[0]
    every_row = lax.all_gather(normed_low, "sub", axis=0, tiled=True)
    piece = lax.all_gather(every_row, "tp", axis=1, tiled=True)
    gate_out = jnp.dot(piece, gate_local, preferred_element_type=jnp.float32)
    up_out = jnp.dot(piece, up_local, preferred_element_type=jnp.float32)
    inner = (jax.nn.silu(gate_out) * up_out).astype(jnp.bfloat16)
    result = jnp.dot(inner, down_local, preferred_element_type=jnp.float32)
    outputs = lax.psum_scatter(result, "tp", scatter_dimension=1, tiled=True)
    returned = lax.all_to_all(outputs, "sub", split_axis=0, concat_axis=0, tiled=True)
    returned = returned.reshape(E, seq_rows, feat_width)
    mixed = jnp.einsum("erc,re->rc", returned, dense)
    return (resid + mixed).astype(jnp.bfloat16)


def solution(mesh):
    in_specs = (
        P(("rep", "sub"), "tp"),
        P(("rep", "sub"), "tp"),
        P(("rep", "sub"), "tp"),
        P(("rep", "sub"), "tp"),
        P(("rep", "sub"), "tp", None),
        P(("rep", "sub"), "tp", None),
        P(("rep", "sub")),
        P("sub", "tp"),
        P("tp"),
        P("tp", None),
        P(("rep", "sub"), None),
        P("sub", None, "tp"),
        P("sub", None, "tp"),
        P("sub", "tp", None),
    )
    out_specs = P(("rep", "sub"), "tp")
    return jax.shard_map(
        on_device, mesh=mesh, in_specs=in_specs, out_specs=out_specs, check_vma=False
    )
```

profile of v0, /device:TPU:0, one launch (start us, length us, event | category | flops | bytes accessed | tf_op | source)
XLA Modules:
  0.0 249.3 jit_solution(16998185043243478273)
XLA Ops:
  6.6 15.8 %all_gather.33 = bf16[16,6144]{1,0:T(8,128)(2,1)S(1)} all-gather(bf16[16,1536]{1,0:T(8,128)(2,1)} %param.17), channel_id=1, replica_groups=mesh['rep'=2,'tp'=4,'sub'=4] {'tp'}, dimensions={1}, use_global_device_ids=true | all-gather | bytes 245760 | tf_op jit(solution)/shard_map/all_gather | solution.py:54
  22.4 0.3 reshape.82
  22.7 13.3 %all_gather.34 = bf16[16,1024]{1,0:T(8,128)(2,1)S(1)} all-gather(bf16[16,256]{1,0:T(8,128)(2,1)} %param.18), channel_id=1, replica_groups=mesh['rep'=2,'tp'=4,'sub'=4] {'tp'}, dimensions={1}, use_global_device_ids=true | all-gather | bytes 40960 | tf_op jit(solution)/shard_map/all_gather | solution.py:55
  36.0 0.7 broadcast_compare_fusion
  36.8 0.3 fusion.40
  37.0 2.0 fusion.39
  39.0 0.4 fusion.19
  39.5 0.8 copy.37
  40.4 0.4 fusion.29
  40.8 15.4 %all-gather.1 = f32[64,8,6]{2,1,0:T(8,128)S(1)} all-gather(f32[16,8,6]{2,1,0:T(8,128)S(1)} %fusion.29), channel_id=3, replica_groups=mesh['rep'=2,'tp'=4,'sub'=4] {'tp'}, dimensions={0}, use_global_device_ids=true | all-gather | bytes 15360 | tf_op jit(solution)/shard_map/all_gather | solution.py:14
  56.2 0.3 copy.43
  56.5 0.1 copy.40
  56.6 16.8 %all-gather = f32[64,8,6]{2,1,0:T(8,128)S(1)} all-gather(f32[16,8,6]{2,1,0:T(8,128)S(1)} %multiply_maximum_fusion), channel_id=2, replica_groups=mesh['rep'=2,'tp'=4,'sub'=4] {'tp'}, dimensions={0}, use_global_device_ids=true | all-gather | bytes 15360 | tf_op jit(solution)/shard_map/all_gather | solution.py:14
  73.5 0.3 copy.42
  73.7 0.1 copy.39
  73.9 13.6 %all_gather.41 = bf16[16,1024]{1,0:T(8,128)(2,1)S(1)} all-gather(bf16[16,256]{1,0:T(8,128)(2,1)} %param.19), channel_id=1, replica_groups=mesh['rep'=2,'tp'=4,'sub'=4] {'tp'}, dimensions={1}, use_global_device_ids=true | all-gather | bytes 40960 | tf_op jit(solution)/shard_map/all_gather | solution.py:56
  87.5 1.0 slice.25
  88.6 5.3 %while.19 = (s32[]{:T(128)}, f32[16,8,6]{0,1,2:T(8,128)S(1)}, f32[16,8,6]{0,1,2:T(8,128)S(1)}, f32[16,8,6,128]{3,2,1,0:T(8,128)S(1)}, f32[4,16,8,6]{1,2,3,0:T(8,...) while((s32[]{:T(128)}, f32[16,8,6]{0,1,2:T(8,128)S(1)}, ...), condition=%wide.region_3.4_spmd, body=%wide.region_2.3_spmd.sunk | while | flops 299525 | bytes 2009239 | solution.py:20
  88.7 0.1 copy.81
  88.8 0.1 copy.82
  89.0 1.0 constant_dynamic-slice_fusion.2
  90.0 0.4 fusion.58
  90.5 0.1 copy.81
  90.6 0.1 copy.82
  90.7 1.0 constant_dynamic-slice_fusion.2
  91.8 0.4 fusion.58
  92.3 0.1 copy.81
  92.5 1.0 constant_dynamic-slice_fusion.2
  93.5 0.4 fusion.58
  94.0 0.1 copy.45
  94.1 0.1 copy.46
  94.3 0.3 divide_convert_fusion
  94.8 7.9 %all_to_all.25 = bf16[16,4,1536]{2,0,1:T(8,128)(2,1)S(1)} all-to-all(bf16[16,4,1536]{2,0,1:T(8,128)(2,1)S(1)} %copy.47), channel_id=1, replica_groups=mesh['rep'=2,'tp'=4,'sub'=4] {'sub'}, dimensions={1} | all-to-all | bytes 393216 | tf_op jit(solution)/shard_map/all_to_all | solution.py:89
  102.7 4.0 %fusion.41 = f32[64,1536]{1,0:T(8,128)} fusion(bf16[64,1536]{1,0:T(8,128)(2,1)S(1)} %bitcast.87, bf16[1536,1536]{1,0:T(8,128)(2,1)} %param.23), kind=kOutput, calls=%fused_computation.62 | convolution fusion | flops 301989888 | bytes 5308416 | tf_op jit(solution)/shard_map/dot_general | solution.py:90
  106.8 21.2 %reduce-scatter.3.cloned.1.call-done = f32[16,1536]{1,0:T(8,128)} async-done(((f32[64,1536]{1,0:T(8,128)}), f32[16,1536]{1,0:T(8,128)}) %reduce-scatter.3.cloned.1.call-update) | async-done | bytes 98320 | tf_op jit(solution)/shard_map/reduce_scatter | solution.py:91
  127.9 1.0 multiply_reduce_fusion
  129.0 11.7 %psum.14 = f32[16]{0:T(128)S(1)} all-reduce(f32[16]{0:T(128)S(1)} %multiply_reduce_fusion), channel_id=1, replica_groups=mesh['rep'=2,'tp'=4,'sub'=4] {'tp'}, use_global_device_ids=true, to_apply=%region_6.7 | all-reduce | flops 16 | bytes 128 | tf_op jit(solution)/shard_map/psum | solution.py:95
  140.7 1.0 fusion.37
  141.7 5.6 %all_gather.42 = bf16[64,1536]{1,0:T(8,128)(2,1)S(1)} all-gather(bf16[16,1536]{1,0:T(8,128)(2,1)S(1)} %get-tuple-element.227), channel_id=1, replica_groups=mesh['rep'=2,'tp'=4,'sub'=4] {'sub'}, dimensions={0}, use_global_device_ids=true | all-gather | bytes 245760 | tf_op jit(solution)/shard_map/all_gather | solution.py:111
  147.3 17.7 %all_gather.43 = bf16[64,6144]{1,0:T(8,128)(2,1)S(1)} all-gather(bf16[64,1536]{1,0:T(8,128)(2,1)S(1)} %all_gather.42), channel_id=1, replica_groups=mesh['rep'=2,'tp'=4,'sub'=4] {'tp'}, dimensions={1}, use_global_device_ids=true | all-gather | bytes 983040 | tf_op jit(solution)/shard_map/all_gather | solution.py:112
  165.0 10.6 %fusion.8 = f32[64,2048]{1,0:T(8,128)S(1)} fusion(bf16[64,6144]{1,0:T(8,128)(2,1)S(1)} %all_gather.43, bf16[1,6144,2048]{2,1,0:T(8,128)(2,1)} %param.27), kind=kOutput, calls=%fused_computation.14 | convolution fusion | flops 1610612736 | bytes 26476544 | tf_op jit(solution)/shard_map/dot_general | solution.py:113
  175.6 21.0 %fusion.4 = f32[64,6144]{1,0:T(8,128)} fusion(bf16[1,2048,6144]{2,1,0:T(8,128)(2,1)} %param.29, bf16[64,6144]{1,0:T(8,128)(2,1)S(1)} %all_gather.43, bf16[1,6144,2048]{2,1,0:T(8,128)(2,1)} %param.28, f32[64,2048]{1,0:T(8,128)S(1)} %fusion.8), kind=kOutput, calls=%fused_computation.10 | convolution fusion | flops 3222011904 | bytes 53215232 | tf_op jit(solution)/shard_map/dot_general | solution.py:116
  196.8 10.7 %psum.15 = f32[16,4]{0,1:T(4,128)S(1)} all-reduce(f32[16,4]{0,1:T(4,128)S(1)} %fusion.42), channel_id=1, replica_groups=mesh['rep'=2,'tp'=4,'sub'=4] {'tp'}, use_global_device_ids=true, to_apply=%region_8.9 | all-reduce | flops 64 | bytes 512 | tf_op jit(solution)/shard_map/psum | solution.py:98
  207.5 23.5 %reduce-scatter.5.cloned.1.call-done = f32[64,1536]{1,0:T(8,128)} async-done(((f32[64,6144]{1,0:T(8,128)}), f32[64,1536]{1,0:T(8,128)}) %reduce-scatter.5.cloned.1.call-update) | async-done | bytes 393232 | tf_op jit(solution)/shard_map/reduce_scatter | solution.py:117
  231.0 3.5 %all-to-all-start.1 = ((f32[4,16,1536]{2,1,0:T(8,128)}), f32[4,16,1536]{2,1,0:T(8,128)S(1)}, u32[]{:S(2)}, u32[]{:S(2)}) async-start(f32[4,16,1536]{2,1,0:T(8,128)} %bitcast.88), calls=%async_computation.3 | async-start | bytes 786432 | tf_op jit(solution)/shard_map/all_to_all | solution.py:118
  234.6 7.2 %all-to-all-done.1 = f32[4,16,1536]{2,1,0:T(8,128)S(1)} async-done(((f32[4,16,1536]{2,1,0:T(8,128)}), f32[4,16,1536]{2,1,0:T(8,128)S(1)}, u32[]{:S(2)}, u32[]{:S(2)}) %all-to-all-start.1) | async-done | bytes 393248 | tf_op jit(solution)/shard_map/all_to_all | solution.py:118
  241.8 0.3 fusion.30
  242.2 0.6 fusion.34
  (44 shorter events, 1.0 us)
Async XLA Ops:
  6.5 32.5 %copy-start = (bf16[16,32,1024]{2,1,0:T(8,128)(2,1)S(1)}, bf16[16,32,1024]{2,1,0:T(8,128)(2,1)}, u32[]{:S(2)}) copy-start(bf16[16,32,1024]{2,1,0:T(8,128)(2,1)} %param.21) | copy-start | bytes 3145732
  6.5 100.2 %copy-start.5 = (bf16[1536]{0:T(1024)(128)(2,1)S(1)}, bf16[1536]{0:T(1024)(128)(2,1)}, u32[]{:S(2)}) copy-start(bf16[1536]{0:T(1024)(128)(2,1)} %param.24) | copy-start | bytes 9220
  6.5 121.4 %copy-start.3 = (bf16[16,1536]{1,0:T(8,128)(2,1)S(1)}, bf16[16,1536]{1,0:T(8,128)(2,1)}, u32[]{:S(2)}) copy-start(bf16[16,1536]{1,0:T(8,128)(2,1)} %param.16) | copy-start | bytes 147460
  6.5 81.0 %all-gather.5.cloned.1.call-start = ((), (), s32[]{:S(2)}) async-start(), calls=%async_computation.6 | async-start | bytes 1966080 | tf_op jit(solution)/shard_map/all_gather | solution.py:14
  40.3 87.6 %reduce-scatter.3.cloned.1.call-start = ((), (), s32[]{:S(2)}) async-start(), calls=%async_computation.4 | async-start | bytes 491520 | tf_op jit(solution)/shard_map/reduce_scatter | solution.py:91
  106.7 124.3 %reduce-scatter.5.cloned.1.call-start = ((), (), s32[]{:S(2)}) async-start(), calls=%async_computation.5 | async-start | bytes 1966080 | tf_op jit(solution)/shard_map/reduce_scatter | solution.py:117
  165.0 77.8 %copy-start.1 = (bf16[16,32,1024]{2,1,0:T(8,128)(2,1)S(1)}, bf16[16,32,1024]{2,1,0:T(8,128)(2,1)}, u32[]{:S(2)}) copy-start(bf16[16,32,1024]{2,1,0:T(8,128)(2,1)} %param.21) | copy-start | bytes 3145732
  175.6 21.1 %copy-start.6 = (s32[16,2]{0,1:T(2,128)S(1)}, s32[16,2]{0,1:T(2,128)}, u32[]{:S(2)}) copy-start(s32[16,2]{0,1:T(2,128)} %param.26) | copy-start | bytes 388
  175.6 21.1 %copy-start.4 = (bf16[1536,4]{0,1:T(4,128)(2,1)S(1)}, bf16[1536,4]{0,1:T(4,128)(2,1)}, u32[]{:S(2)}) copy-start(bf16[1536,4]{0,1:T(4,128)(2,1)} %param.25) | copy-start | bytes 36868
  175.6 66.6 %copy-start.2 = (f32[16,1536]{1,0:T(8,128)S(1)}, f32[16,1536]{1,0:T(8,128)}, u32[]{:S(2)}) copy-start(f32[16,1536]{1,0:T(8,128)} %reduce-scatter.3.cloned.1.call-done) | copy-start | bytes 294916
  231.0 10.8 %all-to-all-start.1 = ((f32[4,16,1536]{2,1,0:T(8,128)}), f32[4,16,1536]{2,1,0:T(8,128)S(1)}, u32[]{:S(2)}, u32[]{:S(2)}) async-start(f32[4,16,1536]{2,1,0:T(8,128)} %bitcast.88), calls=%async_computation.3 | async-start | bytes 786432 | tf_op jit(solution)/shard_map/all_to_all | solution.py:118
Sparse Core Ops, SparseCore 0:
  40.5 43.1 all-gather.4
  106.8 21.0 reduce-scatter.2
  196.8 34.1 reduce-scatter.4
where the time goes:
time: 250 us; the launch traced here: 249 us
  blocking collectives  129 us (52%)
  waiting for transfers between devices  52 us (21%)
  matrix products  38.7 us (15%)
  between operations  13.3 us (5%)
  local copies, waits for them, and re-layouts  7.53 us (3%)
  other arithmetic  5.54 us (2%)
  starting transfers between devices  3.54 us (1%)
    all_gather x2, blocking collectives, combined_all(): everything = jax.tree.map(lambda part: lax.all_gather(part, axis), value)  32.2 us
    reduce_scatter x1, waiting for transfers between devices, on_device(): outputs = lax.psum_scatter(result, 'tp', scatter_dimension=1, tiled=True)  23.5 us
    reduce_scatter x1, waiting for transfers between devices, on_device(): lax.psum_scatter(partial_proj, 'sub', scatter_dimension=0, tiled=True)  21.2 us
    dot_general x1, matrix products, on_device(): result = jnp.dot(inner, down_local, preferred_element_type=jnp.float32)  21 us
    all_gather x1, blocking collectives, on_device(): piece = lax.all_gather(every_row, 'tp', axis=1, tiled=True)  17.7 us
    all_gather x1, blocking collectives, on_device(): lax.all_gather(query, 'tp', axis=1, tiled=True)  15.8 us
    all_gather x1, blocking collectives, on_device(): lax.all_gather(value_new, 'tp', axis=1, tiled=True)  13.6 us
    all_gather x1, blocking collectives, on_device(): lax.all_gather(key_new, 'tp', axis=1, tiled=True)  13.3 us
  transfers between devices with their start and end apart: 4, of which 3 were waited for; matrix products, arithmetic and copies ran while one was open for 1% of the time, Pallas kernels for 0%

commit v1 on v0

--- a/solution.py
+++ b/solution.py
@@ -1,6 +1,11 @@
+import functools
+
 import jax
 import jax.numpy as jnp
+import numpy as np
 from jax import lax
+from jax.experimental import pallas as pl
+from jax.experimental.pallas import tpu as pltpu
 from jax.sharding import PartitionSpec as P
 
 D = 6144
@@ -121,6 +126,380 @@
     return (resid + mixed).astype(jnp.bfloat16)
 
 
+MESH = pl.DeviceIdType.MESH
+HP = 16
+KC = 512
+NEG = -1e30
+
+
+def layer_kernel(
+    n,
+    len_ref, q_ref, kn_ref, vn_ref, hid_ref, gain_ref, rt_ref, routes_ref, kvm_ref, pos_ref, own_ref,
+    kc_hbm, vc_hbm, ow_hbm, gw_hbm, uw_hbm, dw_hbm,
+    out_ref,
+    slots, kc, vc, q_all, o_send, o_recv, st_send, st_recv, att, attn_all, attn_sub,
+    pr_send, pr_recv, resid, hs_send, hs_recv, x_all, f_all, gacc, uacc, inner,
+    y_send, y_recv, z_send, z_recv,
+    slot_sem, kv_sem, send_sem, recv_sem,
+):
+    t = lax.axis_index("tp")
+    s = lax.axis_index("sub")
+    rows, feat = hid_ref.shape
+    local_len = kc.shape[1]
+    kvh = kc.shape[2] // HD
+    hc = feat // HD
+    ff = slots.shape[2]
+    n_slots = slots.shape[0]
+    per_feat = feat // KC
+    n_up = n * per_feat
+    k_down = ff // KC
+    n_down = n * k_down
+    f32, bf16 = jnp.float32, jnp.bfloat16
+
+    def up(d, i):
+        return lax.rem(i + d, n)
+
+    def down(d, i):
+        return lax.rem(i + n - d, n)
+
+    kcopy = pltpu.make_async_copy(kc_hbm, kc, kv_sem.at[0])
+    vcopy = pltpu.make_async_copy(vc_hbm, vc, kv_sem.at[1])
+    kcopy.start()
+    vcopy.start()
+
+    def ow_copy(i):
+        slot = n_slots - per_feat + i
+        return pltpu.make_async_copy(
+            ow_hbm.at[pl.ds(i * KC, KC), :], slots.at[slot, :, pl.ds(0, feat)], slot_sem.at[slot]
+        )
+
+    def up_copy(hbm, k, which):
+        block, part = k // per_feat, lax.rem(k, per_feat)
+        row = pl.multiple_of(up(block, t) * feat + part * KC, KC)
+        return pltpu.make_async_copy(
+            hbm.at[0, pl.ds(row, KC), :], slots.at[2 * k + which], slot_sem.at[2 * k + which]
+        )
+
+    def down_copy(j):
+        block, part = j // k_down, lax.rem(j, k_down)
+        slot = lax.rem(j + n_slots - per_feat, n_slots)
+        col = pl.multiple_of(up(block + 1, t) * feat, 128)
+        row = pl.multiple_of(part * KC, KC)
+        return pltpu.make_async_copy(
+            dw_hbm.at[0, pl.ds(row, KC), pl.ds(col, feat)],
+            slots.at[slot, :, pl.ds(0, feat)],
+            slot_sem.at[slot],
+        )
+
+    for i in range(per_feat):
+        ow_copy(i).start()
+
+    @pl.loop(0, n_up)
+    def _(k):
+        up_copy(gw_hbm, k, 0).start()
+        up_copy(uw_hbm, k, 1).start()
+
+    barrier = pltpu.get_barrier_semaphore()
+    for d in range(1, n):
+        pl.semaphore_signal(barrier, inc=1, device_id={"tp": up(d, t)}, device_id_type=MESH)
+        pl.semaphore_signal(barrier, inc=1, device_id={"sub": up(d, s)}, device_id_type=MESH)
+    pl.semaphore_wait(barrier, 2 * (n - 1))
+
+    def remote(stage, source, target, axis, peer, key, lane, who):
+        return pltpu.make_async_remote_copy(
+            src_ref=source,
+            dst_ref=target,
+            send_sem=send_sem.at[stage, key, lane],
+            recv_sem=recv_sem.at[stage, who, lane],
+            device_id={axis: peer},
+            device_id_type=MESH,
+        )
+
+    pending = []
+
+    def send(stage, source, target, axis, d, lane=0):
+        me = t if axis == "tp" else s
+        copy = remote(stage, source, target, axis, up(d, me), d, lane, me)
+        copy.start()
+        pending.append(copy)
+
+    def arrive(stage, target, axis, who, lane=0):
+        remote(stage, target, target, axis, who, 0, lane, who).wait_recv()
+
+    for d in range(1, n):
+        send(0, q_ref, q_all.at[t], "tp", d)
+    q_all[t] = q_ref[...]
+    kcopy.wait()
+    vcopy.wait()
+    for d in range(1, n):
+        arrive(0, q_all.at[down(d, t)], "tp", down(d, t))
+
+    lanes = lax.broadcasted_iota(jnp.int32, (n * HP, 128), 1)
+    scale = 1.0 / HD**0.5
+    kvm = kvm_ref[...] > 0.5
+    positions = pos_ref[...] + t * local_len
+    own_ok = own_ref[...] == t
+
+    def per_row(b, carry):
+        mx, tot = carry
+        q = q_all[:, b].reshape(n * HP, HD)
+        krow, vrow = kc[b], vc[b]
+        keys = jnp.concatenate([krow[:, g * HD : (g + 1) * HD] for g in range(kvh)], axis=0)
+        vals = jnp.concatenate([vrow[:, g * HD : (g + 1) * HD] for g in range(kvh)], axis=0)
+        dims = (((1,), (1,)), ((), ()))
+        sc = lax.dot_general(q, keys, dims, preferred_element_type=f32) * scale
+        so = lax.dot_general(q, kn_ref[b], dims, preferred_element_type=f32) * scale
+        ok = jnp.logical_and(kvm, positions < len_ref[b])
+        sc = jnp.where(ok, sc, NEG)
+        so = jnp.where(own_ok, so, NEG)
+        m = jnp.maximum(jnp.max(sc, axis=1, keepdims=True), jnp.max(so, axis=1, keepdims=True))
+        p = jnp.where(ok, jnp.exp(sc - m), 0.0)
+        po = jnp.where(own_ok, jnp.exp(so - m), 0.0)
+        l = jnp.sum(p, axis=1, keepdims=True) + jnp.sum(po, axis=1, keepdims=True)
+        o = jnp.dot(p.astype(bf16), vals, preferred_element_type=f32)
+        o = o + jnp.dot(po.astype(bf16), vn_ref[b], preferred_element_type=f32)
+        o_send[:, b] = o.astype(bf16).reshape(n, HP, HD)
+        return jnp.where(lanes == b, m, mx), jnp.where(lanes == b, l, tot)
+
+    zero = jnp.zeros((n * HP, 128), f32)
+    mx, tot = lax.fori_loop(0, rows, per_row, (zero, zero))
+    st_send[:, 0] = mx.reshape(n, HP, 128)
+    st_send[:, 1] = tot.reshape(n, HP, 128)
+
+    for d in range(1, n):
+        send(1, st_send.at[up(d, t)], st_recv.at[t], "tp", d, 1)
+        send(1, o_send.at[up(d, t)], o_recv.at[t], "tp", d)
+    o_recv[t] = o_send[t]
+    st_recv[t] = st_send[t]
+    for d in range(1, n):
+        arrive(1, st_recv.at[down(d, t)], "tp", down(d, t), 1)
+        arrive(1, o_recv.at[down(d, t)], "tp", down(d, t))
+    ms = [st_recv[i, 0] for i in range(n)]
+    best = functools.reduce(jnp.maximum, ms)
+    es = [jnp.exp(m - best) for m in ms]
+    total = sum(es[i] * st_recv[i, 1] for i in range(n))
+    coef = [e / total for e in es]
+    for b in range(rows):
+        att[b] = sum(o_recv[i, b].astype(f32) * coef[i][:, b : b + 1] for i in range(n))
+    for i in range(hc):
+        attn_all[t, :, i * HD : (i + 1) * HD] = att[:, i, :].astype(bf16)
+
+    for d in range(1, n):
+        send(2, attn_all.at[t], attn_all.at[t], "tp", d)
+    chunk_seen = {}
+    for d in range(n):
+        c = down(d, t)
+        if d:
+            arrive(2, attn_all.at[c], "tp", c)
+    for d in range(1, n):
+        send(3, attn_all.at[up(d, s)], attn_sub.at[s], "sub", d)
+    attn_sub[s] = attn_all[s]
+    for i in range(per_feat):
+        ow_copy(i).wait()
+    for d in range(1, n):
+        arrive(3, attn_sub.at[down(d, s)], "sub", down(d, s))
+    a = attn_sub[...].reshape(n * rows, feat)
+    base = n_slots - per_feat
+    proj = jnp.dot(a[:, :KC], slots[base, :, :feat], preferred_element_type=f32)
+    for i in range(1, per_feat):
+        proj += jnp.dot(
+            a[:, i * KC : (i + 1) * KC], slots[base + i, :, :feat], preferred_element_type=f32
+        )
+    pr_send[...] = proj.astype(bf16).reshape(n, rows, feat)
+    for i in range(min(per_feat, n_down)):
+        down_copy(i).start()
+    for d in range(1, n):
+        send(4, pr_send.at[up(d, s)], pr_recv.at[s], "sub", d)
+    pr_recv[s] = pr_send[s]
+    for d in range(1, n):
+        arrive(4, pr_recv.at[down(d, s)], "sub", down(d, s))
+    res = hid_ref[...].astype(f32)
+    for i in range(n):
+        res += pr_recv[i].astype(f32)
+    resid[...] = res
+    hg = res * gain_ref[...]
+    lane16 = lax.broadcasted_iota(jnp.int32, (rows, 128), 1)
+    stat = jnp.where(lane16 == E, jnp.sum(res * res, axis=1, keepdims=True), 0.0)
+    for e in range(E):
+        part = jnp.sum(hg * rt_ref[e : e + 1, :], axis=1, keepdims=True)
+        stat = jnp.where(lane16 == e, part, stat)
+    hs_send[...] = stat
+    x_all[t, s] = hg.astype(bf16)
+
+    for d in range(1, n):
+        send(5, hs_send, hs_recv.at[t], "tp", d, 1)
+        send(5, x_all.at[t, s], x_all.at[t, s], "tp", d)
+    for d in range(1, n):
+        send(6, x_all.at[t, s], x_all.at[t, s], "sub", d, 0)
+    hs_recv[t] = hs_send[...]
+    for d in range(1, n):
+        arrive(5, hs_recv.at[down(d, t)], "tp", down(d, t), 1)
+    summed = sum(hs_recv[i] for i in range(n))
+    rinv = lax.rsqrt(summed[:, E : E + 1] / (n * feat) + 1e-05)
+    logits = summed * rinv
+    first, second = routes_ref[:, 0:1], routes_ref[:, 1:2]
+    first_hot, second_hot = lane16 == first, lane16 == second
+    l1 = jnp.sum(jnp.where(first_hot, logits, 0.0), axis=1, keepdims=True)
+    l2 = jnp.sum(jnp.where(second_hot, logits, 0.0), axis=1, keepdims=True)
+    w1 = 1.0 / (1.0 + jnp.exp(l2 - l1))
+    w2 = 1.0 / (1.0 + jnp.exp(l1 - l2))
+    fin = jnp.where(first_hot, w1, 0.0) + jnp.where(second_hot, w2, 0.0)
+    f_all[s] = jnp.where(lane16 == E, rinv, fin)
+    for d in range(1, n):
+        send(7, f_all.at[s], f_all.at[s], "sub", d)
+    for j in range(1, n):
+        c = down(j, t)
+        arrive(5, x_all.at[c, s], "tp", c)
+        for d in range(1, n):
+            send(6, x_all.at[c, s], x_all.at[c, s], "sub", d, j)
+
+    gacc[...] = jnp.zeros_like(gacc)
+    uacc[...] = jnp.zeros_like(uacc)
+    for block in range(n):
+        c = up(block, t)
+        j = (n - block) % n
+        for d in range(1, n):
+            arrive(6, x_all.at[c, down(d, s)], "sub", down(d, s), j)
+        for part in range(per_feat):
+            k = block * per_feat + part
+            up_copy(gw_hbm, k, 0).wait()
+            up_copy(uw_hbm, k, 1).wait()
+            x = x_all[c, :, :, part * KC : (part + 1) * KC].reshape(n * rows, KC)
+            gacc[...] += jnp.dot(x, slots[2 * k], preferred_element_type=f32)
+            uacc[...] += jnp.dot(x, slots[2 * k + 1], preferred_element_type=f32)
+            for j_down in (per_feat + 2 * k, per_feat + 2 * k + 1):
+                if j_down < n_down:
+                    down_copy(j_down).start()
+    for d in range(1, n):
+        arrive(7, f_all.at[down(d, s)], "sub", down(d, s))
+    facts = f_all[...].reshape(n * rows, 128)
+    rall = facts[:, E : E + 1]
+    mine = lax.broadcasted_iota(jnp.int32, (n * rows, 128), 1) == s
+    share = jnp.sum(jnp.where(mine, facts, 0.0), axis=1, keepdims=True)
+    gate = gacc[...] * rall
+    z = gate / (1.0 + jnp.exp(-gate)) * (uacc[...] * rall)
+    inner[...] = z.astype(bf16)
+
+    def settle(block):
+        for d in range(1, n):
+            who = down(d, s)
+            arrive(8, y_recv.at[block, who], "sub", who, block)
+        y = y_send[block, s].astype(f32)
+        for d in range(1, n):
+            y += y_recv[block, down(d, s)].astype(f32)
+        if block < n - 1:
+            z_send[block] = y.astype(bf16)
+            send(9, z_send.at[block], z_recv.at[t], "tp", block + 1)
+        return y
+
+    for block in range(n):
+        y = None
+        for part in range(k_down):
+            j = block * k_down + part
+            down_copy(j).wait()
+            slot = (j + n_slots - per_feat) % n_slots
+            term = jnp.dot(
+                inner[:, part * KC : (part + 1) * KC],
+                slots[slot, :, :feat],
+                preferred_element_type=f32,
+            )
+            y = term if y is None else y + term
+        y_send[block] = (y * share).astype(bf16).reshape(n, rows, feat)
+        for d in range(1, n):
+            send(8, y_send.at[block, up(d, s)], y_recv.at[block, s], "sub", d, block)
+        if block:
+            settle(block - 1)
+    result = resid[...] + settle(n - 1)
+    for d in range(1, n):
+        who = down(d, t)
+        arrive(9, z_recv.at[who], "tp", who)
+        result += z_recv[who].astype(f32)
+    out_ref[...] = result.astype(bf16)
+    for copy in pending:
+        copy.wait_send()
+
+
+def fused(n, hidden_in, query, key_new, value_new, key_cache, value_cache, lengths, out_weight,
+          norm_gain, router_weight, routes, gate_weight, up_weight, down_weight):
+    rows, feat = hidden_in.shape
+    local_len = key_cache.shape[1]
+    hc, kpc, group = feat // HD, KVH // n, H // KVH
+    ff = gate_weight.shape[2]
+    q3 = jnp.pad(query.reshape(rows, hc, HD), ((0, 0), (0, HP - hc), (0, 0)))
+    kn3 = jnp.pad(key_new.reshape(rows, kpc, HD), ((0, 0), (0, HP - kpc), (0, 0)))
+    vn3 = jnp.pad(value_new.reshape(rows, kpc, HD), ((0, 0), (0, HP - kpc), (0, 0)))
+    head = np.arange(n * HP)
+    chunk, inside = head // HP, head % HP
+    real = inside < hc
+    kv_of = np.where(real, chunk * kpc + inside // group, -1)
+    lane = np.arange(KVH * local_len)
+    kvm = (kv_of[:, None] == (lane // local_len)[None, :]).astype(np.float32)
+    pos = (lane % local_len)[None, :].astype(np.int32)
+    match = real[:, None] & ((inside // group)[:, None] == np.arange(HP)[None, :])
+    own = np.where(match, chunk[:, None], -1).astype(np.int32)
+    bf16, f32 = jnp.bfloat16, jnp.float32
+    per_feat = feat // KC
+    n_slots = 2 * n * per_feat + per_feat
+    vm = pl.BlockSpec(memory_space=pltpu.VMEM)
+    hbm = pl.BlockSpec(memory_space=pl.ANY)
+    sm = pl.BlockSpec(memory_space=pltpu.SMEM)
+    V = pltpu.VMEM
+    return pl.pallas_call(
+        functools.partial(layer_kernel, n),
+        out_shape=jax.ShapeDtypeStruct((rows, feat), bf16),
+        in_specs=[sm] + [vm] * 10 + [hbm] * 6,
+        out_specs=vm,
+        scratch_shapes=[
+            V((n_slots, KC, ff), bf16),
+            V((rows, local_len, KVH * HD), bf16),
+            V((rows, local_len, KVH * HD), bf16),
+            V((n, rows, HP, HD), bf16),
+            V((n, rows, HP, HD), bf16),
+            V((n, rows, HP, HD), bf16),
+            V((n, 2, HP, 128), f32),
+            V((n, 2, HP, 128), f32),
+            V((rows, HP, HD), f32),
+            V((n, rows, feat), bf16),
+            V((n, rows, feat), bf16),
+            V((n, rows, feat), bf16),
+            V((n, rows, feat), bf16),
+            V((rows, feat), f32),
+            V((rows, 128), f32),
+            V((n, rows, 128), f32),
+            V((n, n, rows, feat), bf16),
+            V((n, rows, 128), f32),
+            V((n * rows, ff), f32),
+            V((n * rows, ff), f32),
+            V((n * rows, ff), bf16),
+            V((n, n, rows, feat), bf16),
+            V((n, n, rows, feat), bf16),
+            V((n, rows, feat), bf16),
+            V((n, rows, feat), bf16),
+            pltpu.SemaphoreType.DMA((n_slots,)),
+            pltpu.SemaphoreType.DMA((2,)),
+            pltpu.SemaphoreType.DMA((10, n, n)),
+            pltpu.SemaphoreType.DMA((10, n, n)),
+        ],
+        compiler_params=pltpu.CompilerParams(
+            collective_id=0, has_side_effects=True, vmem_limit_bytes=67043328
+        ),
+    )(
+        lengths, q3, kn3, vn3, hidden_in, norm_gain.astype(f32).reshape(1, feat),
+        router_weight.astype(f32).T, routes, jnp.asarray(kvm), jnp.asarray(pos), jnp.asarray(own),
+        key_cache, value_cache, out_weight, gate_weight, up_weight, down_weight,
+    )
+
+
+def pick(n_tp, n_sub, *args):
+    rows, feat = args[0].shape
+    ff = args[11].shape[2]
+    whole_heads = feat % HD == 0 and KVH % n_tp == 0 and feat // HD <= HP
+    tiles = rows % 16 == 0 and feat % KC == 0 and ff % KC == 0 and feat <= ff
+    if n_tp == n_sub and whole_heads and tiles:
+        return fused(n_tp, *args)
+    return on_device(*args)
+
+
 def solution(mesh):
     in_specs = (
         P(("rep", "sub"), "tp"),
@@ -140,5 +519,5 @@
     )
     out_specs = P(("rep", "sub"), "tp")
     return jax.shard_map(
-        on_device, mesh=mesh, in_specs=in_specs, out_specs=out_specs, check_vma=False
-    )
+        functools.partial(pick, mesh.shape["tp"], mesh.shape["sub"]), mesh=mesh, in_specs=in_specs, out_specs=out_specs, check_vma=False
+    )

time: 250 us -> 89.8 us (0.36)
  blocking collectives: 129 us -> 0 us
  Pallas kernels: 0 us -> 79.8 us
  waiting for transfers between devices: 52 us -> 0 us
  matrix products: 38.7 us -> 0 us
  between operations: 13.3 us -> 0.02 us
  other arithmetic: 5.54 us -> 1.32 us
  starting transfers between devices: 3.54 us -> 0 us
    all_gather x7 -> x0, blocking collectives: 98.3 us -> none  [the longest x2 32.2 us: combined_all(): everything = jax.tree.map(lambda part: lax.all_gather(part, axis), value)]
    pallas_call x0 -> x1, Pallas kernels: none -> 79.8 us  [fused(): pl.pallas_call(functools.partial(layer_kernel, n), out_shape=jax.ShapeDty...]
    reduce_scatter x2 -> x0, waiting for transfers between devices: 44.7 us -> none  [the longest x1 23.5 us: on_device(): outputs = lax.psum_scatter(result, 'tp', scatter_dimension=1, tiled=True)]
    dot_general x8 -> x0, matrix products: 38.7 us -> none  [the longest x1 21 us: on_device(): result = jnp.dot(inner, down_local, preferred_element_type=jnp.float32)]
    psum x2 -> x0, blocking collectives: 22.4 us -> none  [the longest x1 11.7 us: on_device(): squares = lax.psum(jnp.sum(resid * resid, axis=-1), 'tp')]
    all_to_all x1 -> x0, blocking collectives: 7.89 us -> none  [on_device(): lax.all_to_all(attn, 'sub', split_axis=1, concat_axis=0, tiled=True)]
    all_to_all x1 -> x0, waiting for transfers between devices: 7.24 us -> none  [on_device(): lax.all_to_all(outputs, 'sub', split_axis=0, concat_axis=0, tiled=True)]
    all_to_all x1 -> x0, starting transfers between devices: 3.46 us -> none  [on_device(): lax.all_to_all(outputs, 'sub', split_axis=0, concat_axis=0, tiled=True)]
  transfers between devices with their start and end apart: 4 -> 0, of which waited for: 3 -> 0; matrix products, arithmetic and copies ran while one was open for 1% -> 0% of each run, Pallas kernels for 0% -> 0%
where the time goes in v1:
time: 89.8 us; the launch traced here: 89.4 us
  Pallas kernels  79.8 us (89%)
  local copies, waits for them, and re-layouts  8.2 us (9%)
  other arithmetic  1.32 us (1%)
    pallas_call x1, Pallas kernels, fused(): pl.pallas_call(functools.partial(layer_kernel, n), out_shape=jax.ShapeDty...  79.8 us
    unnamed x2, local copies, waits for them, and re-layouts  2.77 us

profile of v1, /device:TPU:0, one launch (start us, length us, event | category | flops | bytes accessed | tf_op | source)
XLA Modules:
  0.0 89.4 jit_solution(4338461489162877783)
XLA Ops:
  0.0 0.8 reshape.14
  0.9 0.6 pad.11.q_ref
  1.5 0.7 reshape.15
  2.2 0.6 pad.12.kn_ref
  2.8 0.7 reshape.16
  3.5 0.6 pad.13.vn_ref
  4.2 1.3 %convert_bitcast_fusion.rt_ref = f32[4,1536]{1,0:T(4,128)} fusion(bf16[1536,4]{0,1:T(4,128)(2,1)} %param.26), kind=kLoop, calls=%fused_computation | loop fusion | flops 6144 | bytes 36864 | tf_op jit(solution)/shard_map/transpose | solution.py:488
  5.5 1.3 %copy.19.routes_ref = s32[16,2]{1,0:T(8,128)} copy(s32[16,2]{0,1:T(2,128)} %param.27) | data formatting | bytes 256 | tf_op args[10]
  6.8 1.3 %reshape.20.gain_ref = f32[1,1536]{1,0:T(1,128)} reshape(bf16[1536]{0:T(1024)(128)(2,1)} %param.25) | data formatting | bytes 9216 | tf_op jit(solution)/shard_map/reshape | solution.py:487
  8.1 79.8 %shard_map.163 = bf16[16,1536]{1,0:T(8,128)(2,1)} custom-call(s32[16]{0:T(128)} %len_ref.1, bf16[16,16,128]{2,1,0:T(8,128)(2,1)} %pad.11.q_ref, bf16[16,16,128]{2,1,0:T(8,128)(2,1)} %pad.12.kn_ref, bf16[16,16,128]{2,1,0:T(8,128)(2,1)} %pad.13.vn_ref, bf16[16,1536]{1,0:T(8,128)(2,1)} %hid_ref.1, f32[1,1536]{1,0:T(1,128)} %reshape.20.gain_ref, ...), custom_call_target="tpu_custom_call" | custom-call | tf_op jit(solution)/shard_map/pallas_call | solution.py:447
  88.0 1.4 %copy.21 = bf16[16,1536]{1,0:T(8,128)(2,1)} copy(bf16[16,1536]{1,0:T(8,128)(2,1)} %shard_map.163) | data formatting | bytes 98304

commit v2 on v1

--- a/solution.py
+++ b/solution.py
@@ -129,6 +129,7 @@
 MESH = pl.DeviceIdType.MESH
 HP = 16
 KC = 512
+HALF = 64
 NEG = -1e30
 
 
@@ -138,7 +139,7 @@
     kc_hbm, vc_hbm, ow_hbm, gw_hbm, uw_hbm, dw_hbm,
     out_ref,
     slots, kc, vc, q_all, o_send, o_recv, st_send, st_recv, att, attn_all, attn_sub,
-    pr_send, pr_recv, resid, hs_send, hs_recv, x_all, f_all, gacc, uacc, inner,
+    qf, knf, vnf, pr_send, pr_recv, resid, hs_send, hs_recv, x_all, f_all, gacc, uacc, inner,
     y_send, y_recv, z_send, z_recv,
     slot_sem, kv_sem, send_sem, recv_sem,
 ):
@@ -162,6 +163,11 @@
     def down(d, i):
         return lax.rem(i + n - d, n)
 
+    barrier = pltpu.get_barrier_semaphore()
+    for d in range(1, n):
+        pl.semaphore_signal(barrier, inc=1, device_id={"tp": up(d, t)}, device_id_type=MESH)
+        pl.semaphore_signal(barrier, inc=1, device_id={"sub": up(d, s)}, device_id_type=MESH)
+
     kcopy = pltpu.make_async_copy(kc_hbm, kc, kv_sem.at[0])
     vcopy = pltpu.make_async_copy(vc_hbm, vc, kv_sem.at[1])
     kcopy.start()
@@ -199,10 +205,6 @@
         up_copy(gw_hbm, k, 0).start()
         up_copy(uw_hbm, k, 1).start()
 
-    barrier = pltpu.get_barrier_semaphore()
-    for d in range(1, n):
-        pl.semaphore_signal(barrier, inc=1, device_id={"tp": up(d, t)}, device_id_type=MESH)
-        pl.semaphore_signal(barrier, inc=1, device_id={"sub": up(d, s)}, device_id_type=MESH)
     pl.semaphore_wait(barrier, 2 * (n - 1))
 
     def remote(stage, source, target, axis, peer, key, lane, who):
@@ -228,11 +230,21 @@
 
     for d in range(1, n):
         send(0, q_ref, q_all.at[t], "tp", d)
+    qf[...] = jnp.zeros_like(qf)
+    knf[...] = jnp.zeros_like(knf)
+    vnf[...] = jnp.zeros_like(vnf)
+    for i in range(kn_ref.shape[1] // HD):
+        knf[:, i, :] = kn_ref[:, i * HD : (i + 1) * HD].astype(f32)
+        vnf[:, i, :] = vn_ref[:, i * HD : (i + 1) * HD].astype(f32)
     q_all[t] = q_ref[...]
+    for d in range(n):
+        c = down(d, t)
+        if d:
+            arrive(0, q_all.at[c], "tp", c)
+        for i in range(hc):
+            qf[c, :, i, :] = q_all[c, :, i * HD : (i + 1) * HD].astype(f32)
     kcopy.wait()
     vcopy.wait()
-    for d in range(1, n):
-        arrive(0, q_all.at[down(d, t)], "tp", down(d, t))
 
     lanes = lax.broadcasted_iota(jnp.int32, (n * HP, 128), 1)
     scale = 1.0 / HD**0.5
@@ -240,15 +252,14 @@
     positions = pos_ref[...] + t * local_len
     own_ok = own_ref[...] == t
 
-    def per_row(b, carry):
-        mx, tot = carry
-        q = q_all[:, b].reshape(n * HP, HD)
+    def per_row(b, stats):
+        q = qf[:, b].reshape(n * HP, HD).astype(bf16)
         krow, vrow = kc[b], vc[b]
         keys = jnp.concatenate([krow[:, g * HD : (g + 1) * HD] for g in range(kvh)], axis=0)
         vals = jnp.concatenate([vrow[:, g * HD : (g + 1) * HD] for g in range(kvh)], axis=0)
         dims = (((1,), (1,)), ((), ()))
         sc = lax.dot_general(q, keys, dims, preferred_element_type=f32) * scale
-        so = lax.dot_general(q, kn_ref[b], dims, preferred_element_type=f32) * scale
+        so = lax.dot_general(q, knf[b].astype(bf16), dims, preferred_element_type=f32) * scale
         ok = jnp.logical_and(kvm, positions < len_ref[b])
         sc = jnp.where(ok, sc, NEG)
         so = jnp.where(own_ok, so, NEG)
@@ -257,14 +268,13 @@
         po = jnp.where(own_ok, jnp.exp(so - m), 0.0)
         l = jnp.sum(p, axis=1, keepdims=True) + jnp.sum(po, axis=1, keepdims=True)
         o = jnp.dot(p.astype(bf16), vals, preferred_element_type=f32)
-        o = o + jnp.dot(po.astype(bf16), vn_ref[b], preferred_element_type=f32)
+        o = o + jnp.dot(po.astype(bf16), vnf[b].astype(bf16), preferred_element_type=f32)
         o_send[:, b] = o.astype(bf16).reshape(n, HP, HD)
-        return jnp.where(lanes == b, m, mx), jnp.where(lanes == b, l, tot)
+        return jnp.where(lanes == b, m, jnp.where(lanes == b + HALF, l, stats))
 
     zero = jnp.zeros((n * HP, 128), f32)
-    mx, tot = lax.fori_loop(0, rows, per_row, (zero, zero))
-    st_send[:, 0] = mx.reshape(n, HP, 128)
-    st_send[:, 1] = tot.reshape(n, HP, 128)
+    stats = lax.fori_loop(0, rows, per_row, zero, unroll=4)
+    st_send[...] = stats.reshape(n, HP, 128)
 
     for d in range(1, n):
         send(1, st_send.at[up(d, t)], st_recv.at[t], "tp", d, 1)
@@ -274,10 +284,10 @@
     for d in range(1, n):
         arrive(1, st_recv.at[down(d, t)], "tp", down(d, t), 1)
         arrive(1, o_recv.at[down(d, t)], "tp", down(d, t))
-    ms = [st_recv[i, 0] for i in range(n)]
+    ms = [st_recv[i] for i in range(n)]
     best = functools.reduce(jnp.maximum, ms)
     es = [jnp.exp(m - best) for m in ms]
-    total = sum(es[i] * st_recv[i, 1] for i in range(n))
+    total = sum(es[i] * pltpu.roll(ms[i], HALF, 1) for i in range(n))
     coef = [e / total for e in es]
     for b in range(rows):
         att[b] = sum(o_recv[i, b].astype(f32) * coef[i][:, b : b + 1] for i in range(n))
@@ -286,13 +296,19 @@
 
     for d in range(1, n):
         send(2, attn_all.at[t], attn_all.at[t], "tp", d)
-    chunk_seen = {}
+
+    def onward(c):
+        return remote(3, attn_all.at[c], attn_sub.at[s], "sub", c, c, 0, s)
+
     for d in range(n):
         c = down(d, t)
         if d:
             arrive(2, attn_all.at[c], "tp", c)
-    for d in range(1, n):
-        send(3, attn_all.at[up(d, s)], attn_sub.at[s], "sub", d)
+
+        @pl.when(c != s)
+        def _():
+            onward(c).start()
+
     attn_sub[s] = attn_all[s]
     for i in range(per_feat):
         ow_copy(i).wait()
@@ -317,11 +333,11 @@
     for i in range(n):
         res += pr_recv[i].astype(f32)
     resid[...] = res
-    hg = res * gain_ref[...]
+    hg = res * gain_ref[...].astype(f32).reshape(1, feat)
     lane16 = lax.broadcasted_iota(jnp.int32, (rows, 128), 1)
     stat = jnp.where(lane16 == E, jnp.sum(res * res, axis=1, keepdims=True), 0.0)
     for e in range(E):
-        part = jnp.sum(hg * rt_ref[e : e + 1, :], axis=1, keepdims=True)
+        part = jnp.sum(hg * rt_ref[e : e + 1, :].astype(f32), axis=1, keepdims=True)
         stat = jnp.where(lane16 == e, part, stat)
     hs_send[...] = stat
     x_all[t, s] = hg.astype(bf16)
@@ -337,7 +353,14 @@
     summed = sum(hs_recv[i] for i in range(n))
     rinv = lax.rsqrt(summed[:, E : E + 1] / (n * feat) + 1e-05)
     logits = summed * rinv
-    first, second = routes_ref[:, 0:1], routes_ref[:, 1:2]
+    square = (rows, rows)
+    eye = lax.broadcasted_iota(jnp.int32, square, 0) == lax.broadcasted_iota(jnp.int32, square, 1)
+
+    def column(i):
+        row = routes_ref[i : i + 1, :].astype(f32)
+        return jnp.sum(jnp.where(eye, row, 0.0), axis=1, keepdims=True).astype(jnp.int32)
+
+    first, second = column(0), column(1)
     first_hot, second_hot = lane16 == first, lane16 == second
     l1 = jnp.sum(jnp.where(first_hot, logits, 0.0), axis=1, keepdims=True)
     l2 = jnp.sum(jnp.where(second_hot, logits, 0.0), axis=1, keepdims=True)
@@ -415,6 +438,8 @@
         arrive(9, z_recv.at[who], "tp", who)
         result += z_recv[who].astype(f32)
     out_ref[...] = result.astype(bf16)
+    for d in range(1, n):
+        onward(up(d, s)).wait_send()
     for copy in pending:
         copy.wait_send()
 
@@ -425,9 +450,6 @@
     local_len = key_cache.shape[1]
     hc, kpc, group = feat // HD, KVH // n, H // KVH
     ff = gate_weight.shape[2]
-    q3 = jnp.pad(query.reshape(rows, hc, HD), ((0, 0), (0, HP - hc), (0, 0)))
-    kn3 = jnp.pad(key_new.reshape(rows, kpc, HD), ((0, 0), (0, HP - kpc), (0, 0)))
-    vn3 = jnp.pad(value_new.reshape(rows, kpc, HD), ((0, 0), (0, HP - kpc), (0, 0)))
     head = np.arange(n * HP)
     chunk, inside = head // HP, head % HP
     real = inside < hc
@@ -453,14 +475,17 @@
             V((n_slots, KC, ff), bf16),
             V((rows, local_len, KVH * HD), bf16),
             V((rows, local_len, KVH * HD), bf16),
+            V((n, rows, feat), bf16),
             V((n, rows, HP, HD), bf16),
             V((n, rows, HP, HD), bf16),
-            V((n, rows, HP, HD), bf16),
-            V((n, 2, HP, 128), f32),
-            V((n, 2, HP, 128), f32),
+            V((n, HP, 128), f32),
+            V((n, HP, 128), f32),
             V((rows, HP, HD), f32),
             V((n, rows, feat), bf16),
             V((n, rows, feat), bf16),
+            V((n, rows, HP, HD), f32),
+            V((rows, HP, HD), f32),
+            V((rows, HP, HD), f32),
             V((n, rows, feat), bf16),
             V((n, rows, feat), bf16),
             V((rows, feat), f32),
@@ -484,8 +509,8 @@
             collective_id=0, has_side_effects=True, vmem_limit_bytes=67043328
         ),
     )(
-        lengths, q3, kn3, vn3, hidden_in, norm_gain.astype(f32).reshape(1, feat),
-        router_weight.astype(f32).T, routes, jnp.asarray(kvm), jnp.asarray(pos), jnp.asarray(own),
+        lengths, query, key_new, value_new, hidden_in, norm_gain,
+        router_weight.T, routes.T, jnp.asarray(kvm), jnp.asarray(pos), jnp.asarray(own),
         key_cache, value_cache, out_weight, gate_weight, up_weight, down_weight,
     )
 
@@ -494,7 +519,7 @@
     rows, feat = args[0].shape
     ff = args[11].shape[2]
     whole_heads = feat % HD == 0 and KVH % n_tp == 0 and feat // HD <= HP
-    tiles = rows % 16 == 0 and feat % KC == 0 and ff % KC == 0 and feat <= ff
+    tiles = rows % 16 == 0 and rows <= HALF and feat % KC == 0 and ff % KC == 0 and feat <= ff
     if n_tp == n_sub and whole_heads and tiles:
         return fused(n_tp, *args)
     return on_device(*args)

time: 89.8 us -> 75.6 us (0.84)
  local copies, waits for them, and re-layouts: 8.2 us -> 1.42 us
  Pallas kernels: 79.8 us -> 74 us
  other arithmetic: 1.32 us -> 0 us
    pallas_call x1, Pallas kernels: 79.8 us -> 74 us  [fused(): pl.pallas_call(functools.partial(layer_kernel, n), out_shape=jax.ShapeDty...]
    reshape x4 -> x0, local copies, waits for them, and re-layouts: 3.54 us -> none  [the longest x1 1.28 us: fused(): norm_gain.astype(f32).reshape(1, feat)]
    pad x3 -> x0, local copies, waits for them, and re-layouts: 1.9 us -> none  [the longest x1 0.64 us: fused(): q3 = jnp.pad(query.reshape(rows, hc, HD), ((0, 0), (0, HP - hc), (0, 0)))]
    unnamed x2 -> x1, local copies, waits for them, and re-layouts: 2.77 us -> 1.42 us
    transpose x1 -> x0, other arithmetic: 1.32 us -> none  [fused(): router_weight.astype(f32)]
where the time goes in v2:
time: 75.6 us; the launch traced here: 75.4 us
  Pallas kernels  74 us (98%)
  local copies, waits for them, and re-layouts  1.42 us (2%)
    pallas_call x1, Pallas kernels, fused(): pl.pallas_call(functools.partial(layer_kernel, n), out_shape=jax.ShapeDty...  74 us

profile of v2, /device:TPU:0, one launch (start us, length us, event | category | flops | bytes accessed | tf_op | source)
XLA Modules:
  0.0 75.4 jit_solution(535956634406550012)
XLA Ops:
  0.0 74.0 %shard_map.163 = bf16[16,1536]{1,0:T(8,128)(2,1)} custom-call(s32[16]{0:T(128)} %len_ref.1, bf16[16,1536]{1,0:T(8,128)(2,1)} %q_ref.1, bf16[16,256]{1,0:T(8,128)(2,1)} %kn_ref.1, bf16[16,256]{1,0:T(8,128)(2,1)} %vn_ref.1, bf16[16,1536]{1,0:T(8,128)(2,1)} %hid_ref.1, bf16[1536]{0:T(1024)(128)(2,1)} %gain_ref.1, bf16[4,1536]{1,0:T(4,128)(2,1)} %bitcast.2, ...), custom_call_target="tpu_custom_call" | custom-call | tf_op jit(solution)/shard_map/pallas_call | solution.py:469
  74.0 1.4 %copy.19 = bf16[16,1536]{1,0:T(8,128)(2,1)} copy(bf16[16,1536]{1,0:T(8,128)(2,1)} %shard_map.163) | data formatting | bytes 98304
